TPU v7x, 32 devices: a whole 2x2x4 slice. The times are simulated.
32 devices in a mesh: kx: 8 (over y, x, core), ky: 4 (over z).
Axes of the slice: x: 2, y: 2, z: 4, core: 2. Of those that a mesh axis runs over, the one named last changes fastest.
Arguments:
- coeffs: bfloat16 [8, 4, 2, 36, 128, 256], P('kx', 'ky'), may hold values from -1 to 1, as said below
- bands: int32 [32], replicated, may hold values from 0 to 35, as said below
- umklapp: int32 [2, 2], replicated, may hold values from -3 to 3
Outputs:
- flux: float32 [8, 4, 2], P('kx', 'ky')
- links: float32 [8, 4, 3, 2], P('kx', 'ky')
Inputs may be any that keep to these rules, and one draw needn't show every extreme that they name: 32 different indices of stored bands. `coeffs`: coefficients of order 1 / sqrt(32768); link matrices between neighbouring k-points stay close enough to unitary that elimination without row exchanges has pivots of magnitude near one.
All inputs are finite; a program needn't handle non-finite values.
Results may differ from a plain program's by a relative error of at most 0.0003.
Values may be sent and summed in bfloat16 or wider, within the bound.
A program may use at most 128 MiB of HBM per device.

v0:
```python
import functools

import jax
import jax.numpy as jnp
from jax import lax
from jax.experimental import pallas as pl
from jax.experimental.pallas import tpu as pltpu
from jax.sharding import PartitionSpec as P

MESH = pl.DeviceIdType.MESH
NT = (((1,), (1,)), ((), ()))
PREP = 8
PIECE = 8


def kernel(
    coeffs, bands_far, umklapp_far, out,
    bands, umklapp, first, rest, plain, local, shifted, upper, left, early, late, early_x, early_d, late_x,
    load_sem, z_send, z_recv, x_send, x_recv, mail_send, mail_recv,
):
    rows, count, cols = plain.shape
    nband = bands.shape[0]
    pieces = rows // PIECE
    nx, ny = lax.axis_size("kx"), lax.axis_size("ky")
    i, j = lax.axis_index("kx"), lax.axis_index("ky")
    i_next, i_prev = lax.rem(i + 1, nx), lax.rem(i + nx - 1, nx)
    j_next, j_prev = lax.rem(j + 1, ny), lax.rem(j + ny - 1, ny)

    load_first = pltpu.make_async_copy(
        coeffs.at[:, :, pl.ds(0, PREP)], first, load_sem.at[0]
    )
    load_rest = pltpu.make_async_copy(
        coeffs.at[:, :, pl.ds(PREP, rows - PREP)], rest, load_sem.at[1]
    )
    load_bands = pltpu.make_async_copy(bands_far, bands, load_sem.at[2])
    load_umklapp = pltpu.make_async_copy(umklapp_far, umklapp, load_sem.at[3])
    load_bands.start()
    load_first.start()
    load_umklapp.start()
    load_rest.start()

    barrier = pltpu.get_barrier_semaphore()
    partners = [
        (i, j_prev), (i, j_next), (i_prev, j), (i_next, j), (i_prev, j_prev), (i_next, j_next),
    ]
    for partner in partners:
        pl.semaphore_signal(barrier, inc=1, device_id=partner, device_id_type=MESH)

    def z_copy(piece):
        span = pl.ds(piece * PIECE, PIECE)
        return pltpu.make_async_remote_copy(
            src_ref=plain.at[span], dst_ref=upper.at[span],
            send_sem=z_send.at[piece], recv_sem=z_recv.at[piece],
            device_id=(i, j_prev), device_id_type=MESH,
        )

    def x_copy(piece):
        span = pl.ds(piece * PIECE, PIECE)
        return pltpu.make_async_remote_copy(
            src_ref=shifted.at[span], dst_ref=left.at[span],
            send_sem=x_send.at[piece], recv_sem=x_recv.at[piece],
            device_id=(i_next, j), device_id_type=MESH,
        )

    def gather(source, start, target):
        picked = [
            source[part, bands[band], pl.ds(start, PREP), :]
            for part in range(2)
            for band in range(nband)
        ]
        block = jnp.stack(picked).astype(jnp.float32)
        plain[pl.ds(target, PREP)] = jnp.swapaxes(block, 0, 1).astype(jnp.bfloat16)

    def send_plain(step):
        for k in range(PREP // PIECE):
            z_copy(step * (PREP // PIECE) + k).start()

    load_bands.wait()
    load_first.wait()
    gather(first, 0, 0)
    pl.semaphore_wait(barrier, len(partners))
    send_plain(0)
    load_rest.wait()
    load_umklapp.wait()

    def gather_step(step, _):
        gather(rest, pl.multiple_of((step - 1) * PREP, PREP), step * PREP)
        send_plain(step)
        return 0

    lax.fori_loop(1, rows // PREP, gather_step, 0)

    off_x = [jnp.where(i == nx - 1, umklapp[0, c], 0) for c in range(2)]
    off_y = [jnp.where(j == ny - 1, umklapp[1, c], 0) for c in range(2)]
    distance = lax.broadcasted_iota(jnp.int32, (cols, cols), 0) - lax.broadcasted_iota(
        jnp.int32, (cols, cols), 1
    )

    def mover(shift):
        far = distance - shift
        hit = (far == 0) | (far == cols) | (far == -cols)
        return jnp.where(hit, 1.0, 0.0).astype(jnp.bfloat16)

    def roll_group(target, start, shift, move):
        block = jnp.concatenate(
            [plain[lax.rem(start + k + shift + rows, rows)] for k in range(4)], axis=0
        )
        moved = jnp.dot(block, move, preferred_element_type=jnp.float32).astype(jnp.bfloat16)
        target[pl.ds(start, 4)] = moved.reshape(4, count, cols)

    move_far = mover(off_x[1] + off_y[1])

    def shift_step(piece, _):
        for k in range(PIECE // 4):
            roll_group(shifted, piece * PIECE + 4 * k, off_x[0] + off_y[0], move_far)
        x_copy(piece).start()
        return 0

    lax.fori_loop(0, pieces, shift_step, 0)
    move_near = mover(off_y[1])

    def local_step(step, _):
        roll_group(local, step * 4, off_y[0], move_near)
        return 0

    lax.fori_loop(0, rows // 4, local_step, 0)

    def left_step(piece, total):
        x_copy(piece).wait_recv()
        for k in range(PIECE):
            row = piece * PIECE + k
            total = total + lax.dot_general(
                left[row], local[row], NT, preferred_element_type=jnp.float32
            )
        return total

    width = 2 * count
    back = width - nband

    def parted(square):
        wide = jnp.concatenate([square, square], axis=1)
        upper_half, lower_half = wide[:nband], wide[nband:]
        return (
            upper_half + pltpu.roll(lower_half, back, 1),
            pltpu.roll(upper_half, back, 1) - lower_half,
        )

    def mail_to(box, slot, index, device):
        return pltpu.make_async_remote_copy(
            src_ref=box, dst_ref=slot, send_sem=mail_send.at[index], recv_sem=mail_recv.at[index],
            device_id=device, device_id_type=MESH,
        )

    total_x = lax.fori_loop(0, pieces, left_step, jnp.zeros((count, count), jnp.float32))
    unit_re, unit_im = det_units(*parted(total_x))
    early[0:1] = unit_re
    early[1:2] = unit_im
    early_to_d = mail_to(early, early_d, 0, (i_prev, j_prev))
    early_to_x = mail_to(early, early_x, 1, (i_prev, j))
    early_to_d.start()
    early_to_x.start()

    def upper_step(piece, total):
        z_copy(piece).wait_recv()
        for k in range(PIECE):
            row = piece * PIECE + k
            lhs = jnp.concatenate([left[row], local[row]], axis=0)
            total = total + lax.dot_general(lhs, upper[row], NT, preferred_element_type=jnp.float32)
        return total

    total = lax.fori_loop(0, pieces, upper_step, jnp.zeros((2 * count, count), jnp.float32))
    lane = lax.broadcasted_iota(jnp.int32, (nband, width), 1)
    d_re, d_im = parted(total[:count])
    y_re, y_im = parted(total[count:])
    unit_re, unit_im = det_units(
        jnp.where(lane < count, d_re, y_re), jnp.where(lane < count, d_im, y_im)
    )
    late[0:1] = unit_re
    late[1:2] = unit_im
    late_to_x = mail_to(late, late_x, 2, (i_prev, j))
    late_to_x.start()

    def drain(piece, _):
        z_copy(piece).wait_send()
        x_copy(piece).wait_send()
        return 0

    lax.fori_loop(0, pieces, drain, 0)
    early_to_x.wait()
    early_to_d.wait()
    along_y = (pltpu.roll(unit_re, count, 1), pltpu.roll(unit_im, count, 1))
    along_x = (early_x[0:1], early_x[1:2])
    x_next = (early_d[0:1], early_d[1:2])
    rest_of_second = times(conjugate(x_next), conjugate(along_y))
    late_to_x.wait()
    late_re, late_im = late_x[0:1], late_x[1:2]
    along_d = (late_re, late_im)
    y_next = (pltpu.roll(late_re, count, 1), pltpu.roll(late_im, count, 1))
    one = times(times(along_x, y_next), conjugate(along_d))
    two = times(along_d, rest_of_second)
    at_zero = lax.broadcasted_iota(jnp.int32, (1, width), 1) == 0
    angle = jnp.arctan2(jnp.where(at_zero, one[1], two[1]), jnp.where(at_zero, one[0], two[0]))
    spot = lax.broadcasted_iota(jnp.int32, (1, width), 1)

    def placed(part):
        return jnp.where(
            spot == 0, along_x[part], jnp.where(spot == 1, along_y[part], along_d[part])
        )

    out[0:1] = angle
    out[1:2] = placed(0)
    out[2:3] = placed(1)
    out[3:8] = jnp.zeros((5, width), jnp.float32)


def split(found, flux, links):
    flux[0] = found[0:1, :2]
    links[0, 0] = found[1:3, :3]


def det_units(work_re, work_im):
    nband, width = work_re.shape
    tiles = nband // 8
    re = [work_re[8 * g : 8 * g + 8] for g in range(tiles)]
    im = [work_im[8 * g : 8 * g + 8] for g in range(tiles)]
    lane8 = lax.broadcasted_iota(jnp.int32, (8, width), 1)
    group_start = lane8 - lax.rem(lane8, nband)
    unit_re = jnp.ones((1, width), jnp.float32)
    unit_im = jnp.zeros((1, width), jnp.float32)
    for k in range(nband):
        g0, r = k // 8, k % 8
        place = group_start + k
        col_re = [jnp.take_along_axis(re[g], place, axis=1) for g in range(g0, tiles)]
        col_im = [jnp.take_along_axis(im[g], place, axis=1) for g in range(g0, tiles)]
        pr, pi = col_re[0][r : r + 1], col_im[0][r : r + 1]
        square = pr * pr + pi * pi
        scale = lax.rsqrt(square)
        nr, ni = pr * scale, pi * scale
        unit_re, unit_im = unit_re * nr - unit_im * ni, unit_re * ni + unit_im * nr
        if k == nband - 1:
            break
        inverse = 1.0 / square
        vr, vi = pr * inverse, -pi * inverse
        row_re, row_im = re[g0][r : r + 1], im[g0][r : r + 1]
        sr = row_re * vr - row_im * vi
        si = row_re * vi + row_im * vr
        for g in range(g0, tiles):
            cr, ci = col_re[g - g0], col_im[g - g0]
            re[g] = re[g] - (cr * sr - ci * si)
            im[g] = im[g] - (cr * si + ci * sr)
    size = 1.0 / jnp.sqrt(unit_re * unit_re + unit_im * unit_im)
    return unit_re * size, unit_im * size


def times(first, second):
    return (
        first[0] * second[0] - first[1] * second[1],
        first[0] * second[1] + first[1] * second[0],
    )


def conjugate(value):
    return (value[0], -value[1])


def per_device(coeffs, bands, umklapp):
    block = coeffs[0, 0]
    rows, cols = block.shape[2], block.shape[3]
    nstore, nband = block.shape[1], bands.shape[0]
    count = 2 * nband
    pieces = rows // PIECE
    side = pltpu.VMEM((rows, count, cols), jnp.bfloat16)
    tile = pltpu.VMEM((8, 2 * count), jnp.float32)
    found = pl.pallas_call(
        kernel,
        out_shape=jax.ShapeDtypeStruct((8, 2 * count), jnp.float32),
        in_specs=[pl.BlockSpec(memory_space=pl.ANY)] * 3,
        out_specs=pl.BlockSpec(memory_space=pltpu.VMEM),
        scratch_shapes=[
            pltpu.SMEM(bands.shape, jnp.int32),
            pltpu.SMEM(umklapp.shape, jnp.int32),
            pltpu.VMEM((2, nstore, PREP, cols), jnp.bfloat16),
            pltpu.VMEM((2, nstore, rows - PREP, cols), jnp.bfloat16),
            side, side, side, side, side,
            tile, tile, tile, tile, tile,
            pltpu.SemaphoreType.DMA((4,)),
            pltpu.SemaphoreType.DMA((pieces,)),
            pltpu.SemaphoreType.DMA((pieces,)),
            pltpu.SemaphoreType.DMA((pieces,)),
            pltpu.SemaphoreType.DMA((pieces,)),
            pltpu.SemaphoreType.DMA((3,)),
            pltpu.SemaphoreType.DMA((3,)),
        ],
        compiler_params=pltpu.CompilerParams(
            collective_id=0, has_side_effects=True, vmem_limit_bytes=63 * 1024 * 1024
        ),
    )(block, bands, umklapp)
    flux, links = pl.pallas_call(
        split,
        out_shape=(
            jax.ShapeDtypeStruct((1, 1, 2), jnp.float32),
            jax.ShapeDtypeStruct((1, 1, 2, 3), jnp.float32),
        ),
        in_specs=[pl.BlockSpec(memory_space=pltpu.VMEM)],
        out_specs=(
            pl.BlockSpec(memory_space=pltpu.VMEM),
            pl.BlockSpec(memory_space=pltpu.VMEM),
        ),
    )(found)
    return (flux, jnp.swapaxes(links, 2, 3))


def solution(mesh):
    in_specs = (P("kx", "ky", None, None, None, None), P(), P())
    out_specs = (P("kx", "ky", None), P("kx", "ky", None, None))
    return jax.shard_map(
        per_device, mesh=mesh, in_specs=in_specs, out_specs=out_specs, check_vma=False
    )
```

profile of v0, /device:TPU:0, one launch (start us, length us, event | category | flops | bytes accessed | tf_op | source)
XLA Modules:
  0.0 104.3 jit_solution(2352237449410164583)
XLA Ops:
  0.6 102.4 %shard_map.50.found = f32[8,128]{1,0:T(8,128)} custom-call(bf16[2,36,128,256]{3,2,1,0:T(8,128)(2,1)} %bitcast.2, s32[32]{0:T(128)} %bands_far.1, s32[2,2]{1,0:T(2,128)} %umklapp_far.1), custom_call_target="tpu_custom_call" | custom-call | tf_op jit(solution)/shard_map/pallas_call | solution.py:274
  103.0 1.2 %shard_map.51 = (f32[1,1,2]{2,1,0:T(1,128)}, f32[1,1,2,3]{3,2,1,0:T(2,128)}) custom-call(f32[8,128]{1,0:T(8,128)} %shard_map.50.found), custom_call_target="tpu_custom_call" | custom-call | tf_op jit(solution)/shard_map/pallas_call | solution.py:298
where the time goes:
time: 105 us; the launch traced here: 104 us
  Pallas kernels  104 us (99%)
    pallas_call x1, Pallas kernels, per_device(): pl.pallas_call(kernel, out_shape=jax.ShapeDtypeStruct((8, 2 * count), jnp...  102 us

commit v1 on v0

--- a/solution.py
+++ b/solution.py
@@ -40,9 +40,7 @@
     load_rest.start()
 
     barrier = pltpu.get_barrier_semaphore()
-    partners = [
-        (i, j_prev), (i, j_next), (i_prev, j), (i_next, j), (i_prev, j_prev), (i_next, j_next),
-    ]
+    partners = [(i, j_prev), (i, j_next), (i_prev, j), (i_next, j)]
     for partner in partners:
         pl.semaphore_signal(barrier, inc=1, device_id=partner, device_id_type=MESH)
 
@@ -50,7 +48,7 @@
         span = pl.ds(piece * PIECE, PIECE)
         return pltpu.make_async_remote_copy(
             src_ref=plain.at[span], dst_ref=upper.at[span],
-            send_sem=z_send.at[piece], recv_sem=z_recv.at[piece],
+            send_sem=z_send.at[0], recv_sem=z_recv.at[piece],
             device_id=(i, j_prev), device_id_type=MESH,
         )
 
@@ -58,7 +56,7 @@
         span = pl.ds(piece * PIECE, PIECE)
         return pltpu.make_async_remote_copy(
             src_ref=shifted.at[span], dst_ref=left.at[span],
-            send_sem=x_send.at[piece], recv_sem=x_recv.at[piece],
+            send_sem=x_send.at[0], recv_sem=x_recv.at[piece],
             device_id=(i_next, j), device_id_type=MESH,
         )
 
@@ -155,10 +153,11 @@
     unit_re, unit_im = det_units(*parted(total_x))
     early[0:1] = unit_re
     early[1:2] = unit_im
-    early_to_d = mail_to(early, early_d, 0, (i_prev, j_prev))
     early_to_x = mail_to(early, early_x, 1, (i_prev, j))
+    early_to_x.start()
+    early_to_x.wait_recv()
+    early_to_d = mail_to(early_x, early_d, 0, (i, j_prev))
     early_to_d.start()
-    early_to_x.start()
 
     def upper_step(piece, total):
         z_copy(piece).wait_recv()
@@ -180,13 +179,15 @@
     late_to_x = mail_to(late, late_x, 2, (i_prev, j))
     late_to_x.start()
 
-    def drain(piece, _):
-        z_copy(piece).wait_send()
-        x_copy(piece).wait_send()
-        return 0
-
-    lax.fori_loop(0, pieces, drain, 0)
-    early_to_x.wait()
+    pltpu.make_async_remote_copy(
+        src_ref=plain, dst_ref=upper, send_sem=z_send.at[0], recv_sem=z_recv.at[0],
+        device_id=(i, j_prev), device_id_type=MESH,
+    ).wait_send()
+    pltpu.make_async_remote_copy(
+        src_ref=shifted, dst_ref=left, send_sem=x_send.at[0], recv_sem=x_recv.at[0],
+        device_id=(i_next, j), device_id_type=MESH,
+    ).wait_send()
+    early_to_x.wait_send()
     early_to_d.wait()
     along_y = (pltpu.roll(unit_re, count, 1), pltpu.roll(unit_im, count, 1))
     along_x = (early_x[0:1], early_x[1:2])
@@ -225,31 +226,46 @@
     im = [work_im[8 * g : 8 * g + 8] for g in range(tiles)]
     lane8 = lax.broadcasted_iota(jnp.int32, (8, width), 1)
     group_start = lane8 - lax.rem(lane8, nband)
-    unit_re = jnp.ones((1, width), jnp.float32)
-    unit_im = jnp.zeros((1, width), jnp.float32)
-    for k in range(nband):
-        g0, r = k // 8, k % 8
-        place = group_start + k
-        col_re = [jnp.take_along_axis(re[g], place, axis=1) for g in range(g0, tiles)]
-        col_im = [jnp.take_along_axis(im[g], place, axis=1) for g in range(g0, tiles)]
-        pr, pi = col_re[0][r : r + 1], col_im[0][r : r + 1]
-        square = pr * pr + pi * pi
-        scale = lax.rsqrt(square)
-        nr, ni = pr * scale, pi * scale
-        unit_re, unit_im = unit_re * nr - unit_im * ni, unit_re * ni + unit_im * nr
-        if k == nband - 1:
-            break
-        inverse = 1.0 / square
-        vr, vi = pr * inverse, -pi * inverse
-        row_re, row_im = re[g0][r : r + 1], im[g0][r : r + 1]
-        sr = row_re * vr - row_im * vi
-        si = row_re * vi + row_im * vr
-        for g in range(g0, tiles):
-            cr, ci = col_re[g - g0], col_im[g - g0]
-            re[g] = re[g] - (cr * sr - ci * si)
-            im[g] = im[g] - (cr * si + ci * sr)
-    size = 1.0 / jnp.sqrt(unit_re * unit_re + unit_im * unit_im)
-    return unit_re * size, unit_im * size
+    unit = (jnp.ones((1, width), jnp.float32), jnp.zeros((1, width), jnp.float32))
+    for g0 in range(tiles):
+        live = range(g0, tiles)
+        cols = []
+        for m in range(8):
+            place = group_start + (8 * g0 + m)
+            cols.append({
+                g: (
+                    jnp.take_along_axis(re[g], place, axis=1),
+                    jnp.take_along_axis(im[g], place, axis=1),
+                )
+                for g in live
+            })
+        for m in range(8):
+            pr, pi = cols[m][g0][0][m : m + 1], cols[m][g0][1][m : m + 1]
+            square = pr * pr + pi * pi
+            scale = lax.rsqrt(square)
+            unit = times(unit, (pr * scale, pi * scale))
+            if 8 * g0 + m == nband - 1:
+                break
+            inverse = 1.0 / square
+            against = {g: times(cols[m][g], (pr, -pi)) for g in live}
+            factor = {g: (against[g][0] * inverse, against[g][1] * inverse) for g in live}
+            for n in range(m + 1, 8):
+                row = (cols[n][g0][0][m : m + 1], cols[n][g0][1][m : m + 1])
+                for g in live:
+                    if n == m + 1 and g == g0:
+                        less = times(against[g], row)
+                        less = (less[0] * inverse, less[1] * inverse)
+                    else:
+                        less = times(factor[g], row)
+                    cols[n][g] = (cols[n][g][0] - less[0], cols[n][g][1] - less[1])
+            if g0 + 1 < tiles:
+                row = (re[g0][m : m + 1], im[g0][m : m + 1])
+                for g in live:
+                    less = times(factor[g], row)
+                    re[g] = re[g] - less[0]
+                    im[g] = im[g] - less[1]
+    size = 1.0 / jnp.sqrt(unit[0] * unit[0] + unit[1] * unit[1])
+    return unit[0] * size, unit[1] * size
 
 
 def times(first, second):
@@ -284,9 +300,9 @@
             side, side, side, side, side,
             tile, tile, tile, tile, tile,
             pltpu.SemaphoreType.DMA((4,)),
+            pltpu.SemaphoreType.DMA((1,)),
             pltpu.SemaphoreType.DMA((pieces,)),
-            pltpu.SemaphoreType.DMA((pieces,)),
-            pltpu.SemaphoreType.DMA((pieces,)),
+            pltpu.SemaphoreType.DMA((1,)),
             pltpu.SemaphoreType.DMA((pieces,)),
             pltpu.SemaphoreType.DMA((3,)),
             pltpu.SemaphoreType.DMA((3,)),

time: 105 us -> 102 us (0.971)
  Pallas kernels: 104 us -> 100 us
    pallas_call x1, Pallas kernels: 102 us -> 99.2 us  [per_device(): pl.pallas_call(kernel, out_shape=jax.ShapeDtypeStruct((8, 2 * count), jnp...]
where the time goes in v1:
time: 102 us; the launch traced here: 101 us
  Pallas kernels  100 us (98%)
    pallas_call x1, Pallas kernels, per_device(): pl.pallas_call(kernel, out_shape=jax.ShapeDtypeStruct((8, 2 * count), jnp...  99.2 us

profile of v1, /device:TPU:0, one launch (start us, length us, event | category | flops | bytes accessed | tf_op | source)
XLA Modules:
  0.0 101.1 jit_solution(8931510693192151708)
XLA Ops:
  0.6 99.2 %shard_map.50.found = f32[8,128]{1,0:T(8,128)} custom-call(bf16[2,36,128,256]{3,2,1,0:T(8,128)(2,1)} %bitcast.2, s32[32]{0:T(128)} %bands_far.1, s32[2,2]{1,0:T(2,128)} %umklapp_far.1), custom_call_target="tpu_custom_call" | custom-call | tf_op jit(solution)/shard_map/pallas_call | solution.py:290
  99.8 1.2 %shard_map.51 = (f32[1,1,2]{2,1,0:T(1,128)}, f32[1,1,2,3]{3,2,1,0:T(2,128)}) custom-call(f32[8,128]{1,0:T(8,128)} %shard_map.50.found), custom_call_target="tpu_custom_call" | custom-call | tf_op jit(solution)/shard_map/pallas_call | solution.py:314

commit v2 on v1

--- a/solution.py
+++ b/solution.py
@@ -289,7 +289,7 @@
     tile = pltpu.VMEM((8, 2 * count), jnp.float32)
     found = pl.pallas_call(
         kernel,
-        out_shape=jax.ShapeDtypeStruct((8, 2 * count), jnp.float32),
+        out_shape=pltpu.VMEM((8, 2 * count), jnp.float32),
         in_specs=[pl.BlockSpec(memory_space=pl.ANY)] * 3,
         out_specs=pl.BlockSpec(memory_space=pltpu.VMEM),
         scratch_shapes=[
@@ -308,7 +308,7 @@
             pltpu.SemaphoreType.DMA((3,)),
         ],
         compiler_params=pltpu.CompilerParams(
-            collective_id=0, has_side_effects=True, vmem_limit_bytes=63 * 1024 * 1024
+            collective_id=0, has_side_effects=True, vmem_limit_bytes=56 * 1024 * 1024
         ),
     )(block, bands, umklapp)
     flux, links = pl.pallas_call(
@@ -322,6 +322,7 @@
             pl.BlockSpec(memory_space=pltpu.VMEM),
             pl.BlockSpec(memory_space=pltpu.VMEM),
         ),
+        compiler_params=pltpu.CompilerParams(vmem_limit_bytes=1024 * 1024),
     )(found)
     return (flux, jnp.swapaxes(links, 2, 3))
 

time: 102 us -> 101 us (level)
  no operation moved by 1% of the time
where the time goes in v2:
time: 101 us; the launch traced here: 99.8 us
  Pallas kernels  99.2 us (98%)
    pallas_call x1, Pallas kernels, per_device(): pl.pallas_call(kernel, out_shape=pltpu.VMEM((8, 2 * count), jnp.float32),...  98.6 us

profile of v2, /device:TPU:0, one launch (start us, length us, event | category | flops | bytes accessed | tf_op | source)
XLA Modules:
  0.0 99.8 jit_solution(16054875746831774091)
XLA Ops:
  0.6 98.6 %shard_map.50.found = f32[8,128]{1,0:T(8,128)S(1)} custom-call(bf16[2,36,128,256]{3,2,1,0:T(8,128)(2,1)} %bitcast.2, s32[32]{0:T(128)} %bands_far.1, s32[2,2]{1,0:T(2,128)} %umklapp_far.1), custom_call_target="tpu_custom_call" | custom-call | tf_op jit(solution)/shard_map/pallas_call | solution.py:290
  99.3 0.6 shard_map.51

commit v3 on v2

--- a/solution.py
+++ b/solution.py
@@ -69,9 +69,16 @@
         block = jnp.stack(picked).astype(jnp.float32)
         plain[pl.ds(target, PREP)] = jnp.swapaxes(block, 0, 1).astype(jnp.bfloat16)
 
-    def send_plain(step):
-        for k in range(PREP // PIECE):
-            z_copy(step * (PREP // PIECE) + k).start()
+    at_once = jnp.where(lax.rem(i, 2) == 0, pieces, 1)
+
+    def send_plain(piece):
+        @pl.when(piece < at_once)
+        def _():
+            z_copy(piece).start()
+
+    def send_late(piece, _):
+        z_copy(piece).start()
+        return 0
 
     load_bands.wait()
     load_first.wait()
@@ -121,7 +128,9 @@
         roll_group(local, step * 4, off_y[0], move_near)
         return 0
 
-    lax.fori_loop(0, rows // 4, local_step, 0)
+    lax.fori_loop(0, rows // 8, local_step, 0)
+    lax.fori_loop(at_once, pieces, send_late, 0)
+    lax.fori_loop(rows // 8, rows // 4, local_step, 0)
 
     def left_step(piece, total):
         x_copy(piece).wait_recv()

time: 101 us -> 99.1 us (0.981); the launches traced: 99.8 us -> 99 us
  no operation moved by 1% of the time
where the time goes in v3:
time: 99.1 us; the launch traced here: 99 us
  Pallas kernels  98.3 us (99%)
    pallas_call x1, Pallas kernels, per_device(): pl.pallas_call(kernel, out_shape=pltpu.VMEM((8, 2 * count), jnp.float32),...  97.8 us

profile of v3, /device:TPU:0, one launch (start us, length us, event | category | flops | bytes accessed | tf_op | source)
XLA Modules:
  0.0 99.0 jit_solution(7943078233260126790)
XLA Ops:
  0.6 97.8 %shard_map.50.found = f32[8,128]{1,0:T(8,128)S(1)} custom-call(bf16[2,36,128,256]{3,2,1,0:T(8,128)(2,1)} %bitcast.2, s32[32]{0:T(128)} %bands_far.1, s32[2,2]{1,0:T(2,128)} %umklapp_far.1), custom_call_target="tpu_custom_call" | custom-call | tf_op jit(solution)/shard_map/pallas_call | solution.py:299
  98.4 0.6 shard_map.51

commit v4 on v3

--- a/solution.py
+++ b/solution.py
@@ -11,6 +11,9 @@
 NT = (((1,), (1,)), ((), ()))
 PREP = 8
 PIECE = 8
+LAST = 2
+X_GROUP = 4
+Z_GROUP = 2
 
 
 def kernel(
@@ -21,6 +24,7 @@
     rows, count, cols = plain.shape
     nband = bands.shape[0]
     pieces = rows // PIECE
+    parts = (PIECE - LAST, LAST)
     nx, ny = lax.axis_size("kx"), lax.axis_size("ky")
     i, j = lax.axis_index("kx"), lax.axis_index("ky")
     i_next, i_prev = lax.rem(i + 1, nx), lax.rem(i + nx - 1, nx)
@@ -40,7 +44,7 @@
     load_rest.start()
 
     barrier = pltpu.get_barrier_semaphore()
-    partners = [(i, j_prev), (i, j_next), (i_prev, j), (i_next, j)]
+    partners = [(i, j_next), (i_prev, j)]
     for partner in partners:
         pl.semaphore_signal(barrier, inc=1, device_id=partner, device_id_type=MESH)
 
@@ -48,15 +52,31 @@
         span = pl.ds(piece * PIECE, PIECE)
         return pltpu.make_async_remote_copy(
             src_ref=plain.at[span], dst_ref=upper.at[span],
-            send_sem=z_send.at[0], recv_sem=z_recv.at[piece],
+            send_sem=z_send.at[0], recv_sem=z_recv.at[2 + piece // Z_GROUP],
             device_id=(i, j_prev), device_id_type=MESH,
+        )
+
+    def z_group(piece, size):
+        span = pl.ds(piece * PIECE, size * PIECE)
+        return pltpu.make_async_remote_copy(
+            src_ref=plain.at[span], dst_ref=upper.at[span],
+            send_sem=z_send.at[0], recv_sem=z_recv.at[2 + piece // Z_GROUP],
+            device_id=(i, j_prev), device_id_type=MESH,
+        )
+
+    def x_group(piece):
+        span = pl.ds(piece * PIECE, X_GROUP * PIECE)
+        return pltpu.make_async_remote_copy(
+            src_ref=shifted.at[span], dst_ref=left.at[span],
+            send_sem=x_send.at[0], recv_sem=x_recv.at[piece // X_GROUP],
+            device_id=(i_next, j), device_id_type=MESH,
         )
 
     def x_copy(piece):
         span = pl.ds(piece * PIECE, PIECE)
         return pltpu.make_async_remote_copy(
             src_ref=shifted.at[span], dst_ref=left.at[span],
-            send_sem=x_send.at[0], recv_sem=x_recv.at[piece],
+            send_sem=x_send.at[0], recv_sem=x_recv.at[piece // X_GROUP],
             device_id=(i_next, j), device_id_type=MESH,
         )
 
@@ -69,7 +89,7 @@
         block = jnp.stack(picked).astype(jnp.float32)
         plain[pl.ds(target, PREP)] = jnp.swapaxes(block, 0, 1).astype(jnp.bfloat16)
 
-    at_once = jnp.where(lax.rem(i, 2) == 0, pieces, 1)
+    at_once = jnp.where(lax.rem(i, 2) == 0, pieces - 1, 1)
 
     def send_plain(piece):
         @pl.when(piece < at_once)
@@ -79,6 +99,14 @@
     def send_late(piece, _):
         z_copy(piece).start()
         return 0
+
+    def z_last(part):
+        span = pl.ds((pieces - 1) * PIECE + part * parts[0], parts[part])
+        return pltpu.make_async_remote_copy(
+            src_ref=plain.at[span], dst_ref=upper.at[span],
+            send_sem=z_send.at[0], recv_sem=z_recv.at[part],
+            device_id=(i, j_prev), device_id_type=MESH,
+        )
 
     load_bands.wait()
     load_first.wait()
@@ -129,11 +157,16 @@
         return 0
 
     lax.fori_loop(0, rows // 8, local_step, 0)
-    lax.fori_loop(at_once, pieces, send_late, 0)
+    lax.fori_loop(at_once, pieces - 1, send_late, 0)
+    z_last(0).start()
+    z_last(1).start()
     lax.fori_loop(rows // 8, rows // 4, local_step, 0)
 
     def left_step(piece, total):
-        x_copy(piece).wait_recv()
+        @pl.when(lax.rem(piece, X_GROUP) == 0)
+        def _():
+            x_group(piece).wait_recv()
+
         for k in range(PIECE):
             row = piece * PIECE + k
             total = total + lax.dot_general(
@@ -168,20 +201,33 @@
     early_to_d = mail_to(early_x, early_d, 0, (i, j_prev))
     early_to_d.start()
 
+    def add_row(row, total):
+        sides = jnp.concatenate([left[row], local[row]], axis=0)
+        return total + lax.dot_general(upper[row], sides, NT, preferred_element_type=jnp.float32)
+
+    whole = (pieces - 1) // Z_GROUP * Z_GROUP
+
     def upper_step(piece, total):
-        z_copy(piece).wait_recv()
+        @pl.when((lax.rem(piece, Z_GROUP) == 0) & (piece < whole))
+        def _():
+            z_group(piece, Z_GROUP).wait_recv()
+
+        @pl.when(piece == whole)
+        def _():
+            z_group(piece, pieces - 1 - whole).wait_recv()
+
         for k in range(PIECE):
-            row = piece * PIECE + k
-            lhs = jnp.concatenate([left[row], local[row]], axis=0)
-            total = total + lax.dot_general(lhs, upper[row], NT, preferred_element_type=jnp.float32)
+            total = add_row(piece * PIECE + k, total)
         return total
 
-    total = lax.fori_loop(0, pieces, upper_step, jnp.zeros((2 * count, count), jnp.float32))
-    lane = lax.broadcasted_iota(jnp.int32, (nband, width), 1)
-    d_re, d_im = parted(total[:count])
-    y_re, y_im = parted(total[count:])
+    total = lax.fori_loop(0, pieces - 1, upper_step, jnp.zeros((count, width), jnp.float32))
+    for part in range(2):
+        z_last(part).wait_recv()
+        for k in range(parts[part]):
+            total = add_row((pieces - 1) * PIECE + part * parts[0] + k, total)
+    over, under = total[:nband], total[nband:]
     unit_re, unit_im = det_units(
-        jnp.where(lane < count, d_re, y_re), jnp.where(lane < count, d_im, y_im)
+        over + pltpu.roll(under, back, 1), under - pltpu.roll(over, back, 1)
     )
     late[0:1] = unit_re
     late[1:2] = unit_im
@@ -202,7 +248,7 @@
     along_x = (early_x[0:1], early_x[1:2])
     x_next = (early_d[0:1], early_d[1:2])
     rest_of_second = times(conjugate(x_next), conjugate(along_y))
-    late_to_x.wait()
+    late_to_x.wait_recv()
     late_re, late_im = late_x[0:1], late_x[1:2]
     along_d = (late_re, late_im)
     y_next = (pltpu.roll(late_re, count, 1), pltpu.roll(late_im, count, 1))
@@ -221,6 +267,7 @@
     out[1:2] = placed(0)
     out[2:3] = placed(1)
     out[3:8] = jnp.zeros((5, width), jnp.float32)
+    late_to_x.wait_send()
 
 
 def split(found, flux, links):
@@ -310,9 +357,9 @@
             tile, tile, tile, tile, tile,
             pltpu.SemaphoreType.DMA((4,)),
             pltpu.SemaphoreType.DMA((1,)),
-            pltpu.SemaphoreType.DMA((pieces,)),
+            pltpu.SemaphoreType.DMA((2 + pieces // Z_GROUP,)),
             pltpu.SemaphoreType.DMA((1,)),
-            pltpu.SemaphoreType.DMA((pieces,)),
+            pltpu.SemaphoreType.DMA((pieces // X_GROUP,)),
             pltpu.SemaphoreType.DMA((3,)),
             pltpu.SemaphoreType.DMA((3,)),
         ],

time: 99.1 us -> 98.8 us (level)
  no operation moved by 1% of the time
where the time goes in v4:
time: 98.8 us; the launch traced here: 98.6 us
  Pallas kernels  98 us (99%)
    pallas_call x1, Pallas kernels, per_device(): pl.pallas_call(kernel, out_shape=pltpu.VMEM((8, 2 * count), jnp.float32),...  97.4 us

profile of v4, /device:TPU:0, one launch (start us, length us, event | category | flops | bytes accessed | tf_op | source)
XLA Modules:
  0.0 98.6 jit_solution(6377780251620527356)
XLA Ops:
  0.6 97.4 %shard_map.50.found = f32[8,128]{1,0:T(8,128)S(1)} custom-call(bf16[2,36,128,256]{3,2,1,0:T(8,128)(2,1)} %bitcast.2, s32[32]{0:T(128)} %bands_far.1, s32[2,2]{1,0:T(2,128)} %umklapp_far.1), custom_call_target="tpu_custom_call" | custom-call | tf_op jit(solution)/shard_map/pallas_call | solution.py:346
  98.1 0.6 shard_map.51

commit v5 on v4

--- a/solution.py
+++ b/solution.py
@@ -38,15 +38,15 @@
     )
     load_bands = pltpu.make_async_copy(bands_far, bands, load_sem.at[2])
     load_umklapp = pltpu.make_async_copy(umklapp_far, umklapp, load_sem.at[3])
+    barrier = pltpu.get_barrier_semaphore()
+    partners = [(i, j_next), (i_prev, j)]
+    for partner in partners:
+        pl.semaphore_signal(barrier, inc=1, device_id=partner, device_id_type=MESH)
+
     load_bands.start()
     load_first.start()
     load_umklapp.start()
     load_rest.start()
-
-    barrier = pltpu.get_barrier_semaphore()
-    partners = [(i, j_next), (i_prev, j)]
-    for partner in partners:
-        pl.semaphore_signal(barrier, inc=1, device_id=partner, device_id_type=MESH)
 
     def z_copy(piece):
         span = pl.ds(piece * PIECE, PIECE)
@@ -285,6 +285,9 @@
     unit = (jnp.ones((1, width), jnp.float32), jnp.zeros((1, width), jnp.float32))
     for g0 in range(tiles):
         live = range(g0, tiles)
+        if g0 == tiles - 1:
+            size = 1.0 / jnp.sqrt(unit[0] * unit[0] + unit[1] * unit[1])
+            unit = (unit[0] * size, unit[1] * size)
         cols = []
         for m in range(8):
             place = group_start + (8 * g0 + m)
@@ -320,8 +323,7 @@
                     less = times(factor[g], row)
                     re[g] = re[g] - less[0]
                     im[g] = im[g] - less[1]
-    size = 1.0 / jnp.sqrt(unit[0] * unit[0] + unit[1] * unit[1])
-    return unit[0] * size, unit[1] * size
+    return unit
 
 
 def times(first, second):

time: 98.8 us -> 98.8 us (level)
  no operation moved by 1% of the time
where the time goes in v5:
time: 98.8 us; the launch traced here: 98.6 us
  Pallas kernels  98 us (99%)
    pallas_call x1, Pallas kernels, per_device(): pl.pallas_call(kernel, out_shape=pltpu.VMEM((8, 2 * count), jnp.float32),...  97.4 us

profile of v5, /device:TPU:0, one launch (start us, length us, event | category | flops | bytes accessed | tf_op | source)
XLA Modules:
  0.0 98.6 jit_solution(3260058659241627153)
XLA Ops:
  0.6 97.4 %shard_map.50.found = f32[8,128]{1,0:T(8,128)S(1)} custom-call(bf16[2,36,128,256]{3,2,1,0:T(8,128)(2,1)} %bitcast.2, s32[32]{0:T(128)} %bands_far.1, s32[2,2]{1,0:T(2,128)} %umklapp_far.1), custom_call_target="tpu_custom_call" | custom-call | tf_op jit(solution)/shard_map/pallas_call | solution.py:348
  98.0 0.6 shard_map.51

commit v6 on v5

--- a/solution.py
+++ b/solution.py
@@ -226,11 +226,12 @@
         for k in range(parts[part]):
             total = add_row((pieces - 1) * PIECE + part * parts[0] + k, total)
     over, under = total[:nband], total[nband:]
-    unit_re, unit_im = det_units(
-        over + pltpu.roll(under, back, 1), under - pltpu.roll(over, back, 1)
-    )
-    late[0:1] = unit_re
-    late[1:2] = unit_im
+    unit_d, along_y = det_units(
+        over + pltpu.roll(under, back, 1), under - pltpu.roll(over, back, 1), (0, count)
+    )
+    for part in range(2):
+        late[part : part + 1] = unit_d[part]
+        late[2 + part : 3 + part] = along_y[part]
     late_to_x = mail_to(late, late_x, 2, (i_prev, j))
     late_to_x.start()
 
@@ -244,14 +245,12 @@
     ).wait_send()
     early_to_x.wait_send()
     early_to_d.wait()
-    along_y = (pltpu.roll(unit_re, count, 1), pltpu.roll(unit_im, count, 1))
     along_x = (early_x[0:1], early_x[1:2])
     x_next = (early_d[0:1], early_d[1:2])
     rest_of_second = times(conjugate(x_next), conjugate(along_y))
     late_to_x.wait_recv()
-    late_re, late_im = late_x[0:1], late_x[1:2]
-    along_d = (late_re, late_im)
-    y_next = (pltpu.roll(late_re, count, 1), pltpu.roll(late_im, count, 1))
+    along_d = (late_x[0:1], late_x[1:2])
+    y_next = (late_x[2:3], late_x[3:4])
     one = times(times(along_x, y_next), conjugate(along_d))
     two = times(along_d, rest_of_second)
     at_zero = lax.broadcasted_iota(jnp.int32, (1, width), 1) == 0
@@ -275,7 +274,7 @@
     links[0, 0] = found[1:3, :3]
 
 
-def det_units(work_re, work_im):
+def det_units(work_re, work_im, starts=None):
     nband, width = work_re.shape
     tiles = nband // 8
     re = [work_re[8 * g : 8 * g + 8] for g in range(tiles)]
@@ -288,6 +287,8 @@
         if g0 == tiles - 1:
             size = 1.0 / jnp.sqrt(unit[0] * unit[0] + unit[1] * unit[1])
             unit = (unit[0] * size, unit[1] * size)
+            if starts is not None:
+                return [last_panel(re[g0], im[g0], unit, lane8 * 0 + start, nband) for start in starts]
         cols = []
         for m in range(8):
             place = group_start + (8 * g0 + m)
@@ -324,6 +325,32 @@
                     re[g] = re[g] - less[0]
                     im[g] = im[g] - less[1]
     return unit
+
+
+def last_panel(re, im, unit, start, nband):
+    def spread(value, place):
+        return jnp.take_along_axis(value, place, axis=1)
+
+    cols = [(spread(re, start + nband - 8 + m), spread(im, start + nband - 8 + m)) for m in range(8)]
+    unit = tuple(spread(jnp.broadcast_to(part, re.shape), start)[0:1] for part in unit)
+    for m in range(8):
+        pr, pi = cols[m][0][m : m + 1], cols[m][1][m : m + 1]
+        square = pr * pr + pi * pi
+        scale = lax.rsqrt(square)
+        unit = times(unit, (pr * scale, pi * scale))
+        if m == 7:
+            return unit
+        inverse = 1.0 / square
+        against = times(cols[m], (pr, -pi))
+        factor = (against[0] * inverse, against[1] * inverse)
+        for n in range(m + 1, 8):
+            row = (cols[n][0][m : m + 1], cols[n][1][m : m + 1])
+            if n == m + 1:
+                less = times(against, row)
+                less = (less[0] * inverse, less[1] * inverse)
+            else:
+                less = times(factor, row)
+            cols[n] = (cols[n][0] - less[0], cols[n][1] - less[1])
 
 
 def times(first, second):

time: 98.8 us -> 98.8 us (level)
  no operation moved by 1% of the time
where the time goes in v6:
time: 98.8 us; the launch traced here: 98.6 us
  Pallas kernels  98 us (99%)
    pallas_call x1, Pallas kernels, per_device(): pl.pallas_call(kernel, out_shape=pltpu.VMEM((8, 2 * count), jnp.float32),...  97.4 us

profile of v6, /device:TPU:0, one launch (start us, length us, event | category | flops | bytes accessed | tf_op | source)
XLA Modules:
  0.0 98.6 jit_solution(1144003042084162305)
XLA Ops:
  0.6 97.4 %shard_map.50.found = f32[8,128]{1,0:T(8,128)S(1)} custom-call(bf16[2,36,128,256]{3,2,1,0:T(8,128)(2,1)} %bitcast.2, s32[32]{0:T(128)} %bands_far.1, s32[2,2]{1,0:T(2,128)} %umklapp_far.1), custom_call_target="tpu_custom_call" | custom-call | tf_op jit(solution)/shard_map/pallas_call | solution.py:375
  98.0 0.6 shard_map.51
